TPU v7x, 32 devices: a whole 2x2x4 slice. The times are simulated.
32 devices in a mesh: node: 8 (over z, y), rep: 4 (over x, core).
Axes of the slice: x: 2, y: 2, z: 4, core: 2. Of those that a mesh axis runs over, the one named last changes fastest.
Arguments:
- coords: float32 [3, 4096], P(None, 'node'), may hold values from 0 to 2, as said below
- omega: bfloat16 [4096, 512], P('node', 'rep'), may hold values from -6 to 6
- skeleton: int32 [8, 256], P('node', 'rep'), may hold values from 0 to 4095, as said below
Outputs:
- row_sample: bfloat16 [4096, 512], P('node', 'rep')
- col_sample: float32 [4096, 512], P('node', 'rep')
Inputs may be any that keep to these rules, and one draw needn't show every extreme that they name: `skeleton`: each node's list holds distinct indices, none inside its own points, at most 73 inside the points of any one other node; in every draw one node's points hold exactly 73 indices of every other node's list. `coords`: the first coordinate of point p lies between 2 (p // 512) / 8 and 2 (p // 512 + 1) / 8; the other two lie in [0, 1].
All inputs are finite; a program needn't handle non-finite values.
Results may differ from a plain program's by a relative error of at most 0.0049.
Values may be sent and summed in bfloat16 or wider, within the bound.
A program may use at most 128 MiB of HBM per device.

v0:
```python
import functools

import jax
import jax.numpy as jnp
from jax import lax
from jax.experimental import pallas as pl
from jax.experimental.pallas import tpu as pltpu
from jax.sharding import PartitionSpec as P

kernel_scale = 0.0078125
softening = 0.02
f32, bf16 = jnp.float32, jnp.bfloat16
MESH = pl.DeviceIdType.MESH


def each(start, stop, body):
    if stop - start <= 8:
        for i in range(start, stop):
            body(i)
    else:
        lax.fori_loop(start, stop, lambda i, c: (body(i), c)[1], 0)


def far_first(n, body):
    half = n // 2
    if n <= 16:
        for d in sorted(range(1, n), key=lambda d: (abs(d - half), d)):
            body(d)
    else:
        each(0, n - 1, lambda d: body(1 + lax.rem(d + half - 1, n - 1)))


def tile(col, row):
    squared = (col[:, 0:1] - row[0:1, :]) ** 2
    squared = squared + (col[:, 1:2] - row[1:2, :]) ** 2
    squared = squared + (col[:, 2:3] - row[2:3, :]) ** 2
    return (kernel_scale * lax.rsqrt(squared + softening * softening)).astype(bf16)


def dot(a, b):
    return jnp.dot(a, b, preferred_element_type=f32)


def kernel(n, reps, cap, coords_in, omega_in, skel_in, row_out, col_out,
           coords, omega, skel, loaded, lists, points, side, keyed, local_req, local_own, rows_out, rows_in, prod_out, prod_in,
           pick_own, far_tile, total,
           list_send, list_recv, point_send, point_recv, side_send, side_recv,
           rows_send, rows_recv, prod_send, prod_recv):
    leaf = coords.shape[1]
    piece = skel.shape[1]
    rank = piece * reps
    me, my_rep = lax.axis_index("node"), lax.axis_index("rep")
    flat = me * reps + my_rep
    count = n * reps

    def at(node, rep):
        return {"node": node, "rep": rep}

    def other(d):
        t = lax.rem(flat + d, count)
        return lax.div(t, reps), lax.rem(t, reps)

    barrier = pltpu.get_barrier_semaphore()

    def greet(d):
        node, rep = other(d)
        pl.semaphore_signal(barrier, inc=1, device_id=at(node, rep), device_id_type=MESH)

    each(1, count, greet)

    loads = [pltpu.make_async_copy(a, b, loaded.at[i]) for i, (a, b) in
             enumerate(((coords_in, coords), (omega_in, omega), (skel_in, skel)))]
    for load in loads:
        load.start()
    for load in loads:
        load.wait()
    own_points = coords[...]
    own_cols = jnp.transpose(jnp.concatenate([own_points, jnp.zeros((5, leaf), f32)], axis=0))
    total[...] = dot(tile(own_cols, own_points), omega[...])
    points[me] = own_points
    lists[my_rep, pl.ds(me, 1)] = skel[...]
    rows_in[me] = jnp.zeros((cap, omega.shape[1]), bf16)
    prod_in[me] = jnp.zeros((cap, omega.shape[1]), bf16)

    pl.semaphore_wait(barrier, count - 1)

    def list_copy(d, node, rep, index):
        return pltpu.make_async_remote_copy(
            src_ref=skel, dst_ref=lists.at[my_rep, pl.ds(me, 1)],
            send_sem=list_send.at[d], recv_sem=list_recv.at[index],
            device_id=at(node, rep), device_id_type=MESH)

    def list_arrival(d):
        node, rep = other(d)
        return pltpu.make_async_remote_copy(
            src_ref=skel, dst_ref=lists.at[rep, pl.ds(node, 1)],
            send_sem=list_send.at[d], recv_sem=list_recv.at[node * reps + rep],
            device_id=at(node, rep), device_id_type=MESH)

    def start_list(d):
        node, rep = other(d)
        list_copy(d, node, rep, flat).start()

    each(1, count, start_list)

    def exchange(d, back, src, dst, send, recv):
        peer = lax.rem(me + d, n)
        place = peer if back else me
        return pltpu.make_async_remote_copy(
            src_ref=src(peer), dst_ref=dst.at[place], send_sem=send.at[peer],
            recv_sem=recv.at[place], device_id=at(peer, my_rep), device_id_type=MESH)

    point_x = lambda d, back=False: exchange(d, back, lambda peer: coords, points, point_send, point_recv)
    rows_x = lambda d, back=False: exchange(d, back, lambda peer: rows_out.at[peer], rows_in, rows_send, rows_recv)
    prod_x = lambda d, back=False: exchange(d, back, lambda peer: prod_out.at[peer], prod_in, prod_send, prod_recv)

    each(1, n, lambda d: point_x(d).start())

    def side_copy(slot):
        peer = me + (1 if slot == 0 else -1)
        return pltpu.make_async_remote_copy(
            src_ref=omega, dst_ref=side.at[slot], send_sem=side_send.at[slot],
            recv_sem=side_recv.at[slot], device_id=at(peer, my_rep), device_id_type=MESH)

    has_above, has_below = me < n - 1, me > 0

    @pl.when(has_above)
    def _():
        side_copy(0).start()

    @pl.when(has_below)
    def _():
        side_copy(1).start()

    each(1, count, lambda d: list_arrival(d).wait_recv())

    listed = jnp.concatenate([lists[r] for r in range(reps)], axis=1)
    mine = jnp.concatenate([lists[r, pl.ds(me, 1)] for r in range(reps)], axis=1)
    local_own[...] = lax.rem(listed, leaf).astype(f32)
    local_req[...] = lax.rem(mine, leaf).astype(f32)
    hit_req = lax.div(mine, leaf) == lax.broadcasted_iota(jnp.int32, (n, rank), 0)
    hit_own = lax.div(listed, leaf) == me
    before = (lax.broadcasted_iota(jnp.int32, (rank, rank), 0)
              < lax.broadcasted_iota(jnp.int32, (rank, rank), 1)).astype(f32).astype(bf16)
    keyed[0] = jnp.where(hit_req, dot(hit_req.astype(f32).astype(bf16), before), -1.0)
    keyed[1] = jnp.where(hit_own, dot(hit_own.astype(f32).astype(bf16), before), -1.0)

    slot_ids = lax.broadcasted_iota(jnp.int32, (cap, rank), 0).astype(f32)
    leaf_ids = lax.broadcasted_iota(jnp.int32, (cap, leaf), 1).astype(f32)

    def picker(keys, local):
        found = jnp.sum(jnp.where(keys == slot_ids, local + 1.0, 0.0), axis=1, keepdims=True)
        return jnp.where(found - 1.0 == leaf_ids, 1.0, 0.0).astype(bf16)

    def send_rows(d):
        peer = lax.rem(me + d, n)
        pick = picker(keyed[1, pl.ds(peer, 1)], local_own[pl.ds(peer, 1)])
        pick_own[peer] = pick
        rows_out[peer] = dot(pick, omega[...]).astype(bf16)
        rows_x(d).start()

    def send_products(d):
        peer = lax.rem(me + d, n)
        point_x(d, True).wait_recv()
        pick = picker(keyed[0, pl.ds(peer, 1)], local_req[...])
        whole = points[peer]
        high = whole.astype(bf16).astype(f32)
        middle = (whole - high).astype(bf16).astype(f32)
        low = whole - high - middle
        parts = jnp.concatenate([high, middle, low], axis=0).astype(bf16)
        got = lax.dot_general(pick, parts, (((1,), (1,)), ((), ())), preferred_element_type=f32)
        slots = got[:, 0:3] + got[:, 3:6] + got[:, 6:9]
        skel_tile = tile(slots, own_points)
        far_tile[peer] = skel_tile
        prod_out[peer] = dot(skel_tile, omega[...]).astype(bf16)
        prod_x(d).start()

    far_first(n, send_rows)
    pick_own[me] = jnp.zeros((cap, leaf), bf16)
    far_tile[me] = jnp.zeros((cap, leaf), bf16)
    far_first(n, send_products)

    @pl.when(has_below)
    def _():
        side_copy(0).wait_recv()
        total[...] += dot(tile(own_cols, points[jnp.maximum(me - 1, 0)]), side[0])

    @pl.when(has_above)
    def _():
        side_copy(1).wait_recv()
        total[...] += dot(tile(own_cols, points[jnp.minimum(me + 1, n - 1)]), side[1])

    far = far_tile[...].reshape(n * cap, leaf).T
    back = pick_own[...].reshape(n * cap, leaf).T

    each(1, n, lambda d: rows_x(d, True).wait_recv())
    row_out[...] = (total[...] + dot(far, rows_in[...].reshape(n * cap, -1)))
    each(1, n, lambda d: prod_x(d, True).wait_recv())
    col_out[...] = dot(back, prod_in[...].reshape(n * cap, -1))

    each(1, count, lambda d: list_arrival(d).wait_send())
    each(1, n, lambda d: point_x(d).wait_send())
    each(1, n, lambda d: rows_x(d).wait_send())
    each(1, n, lambda d: prod_x(d).wait_send())

    @pl.when(has_above)
    def _():
        side_copy(0).wait_send()

    @pl.when(has_below)
    def _():
        side_copy(1).wait_send()


def near_kernel(n, reps, cap, sent, coords_in, omega_in, skel_in, row_out, col_out,
                coords, omega, skel, lists, points, side, rows_out, rows_in, prod_out,
                prod_in, pick_own, pick_req, far_tile, total,
                loaded, piece_send, piece_recv, list_send, list_recv, point_send, point_recv,
                side_send, side_recv, rows_send, rows_recv, prod_send, prod_recv, above, below):
    leaf, samp = omega.shape
    rank = skel.shape[1] * reps
    me, my_rep = lax.axis_index("node"), lax.axis_index("rep")
    close = (-2, -1, 1, 2)
    distant = [o * sign for o in sorted(range(3, n), key=lambda o: abs(o - n // 2)) for sign in (1, -1)]
    place = {o: k for k, o in enumerate(close)}

    def if_there(offset, body):
        @pl.when(me + offset < n if offset > 0 else me + offset >= 0)
        def _():
            body()

    def signal(sem, node, rep):
        pl.semaphore_signal(sem, inc=1, device_id={"node": node, "rep": rep}, device_id_type=MESH)

    def send(src, dst, send_sem, recv_sem, node, rep):
        return pltpu.make_async_remote_copy(
            src_ref=src, dst_ref=dst, send_sem=send_sem, recv_sem=recv_sem,
            device_id={"node": node, "rep": rep}, device_id_type=MESH)

    def exchange(offset, back, src, dst, send_sems, recv_sems):
        peer = me + offset
        spot = peer if back else me
        return send(src(peer), dst(spot), send_sems.at[peer], recv_sems.at[spot], peer, my_rep)

    def point_x(o, back=False):
        return exchange(o, back, lambda p: coords, lambda p: points.at[p], point_send, point_recv)

    def list_x(o, k, back=False):
        rep, peer = lax.rem(my_rep + k, reps), me + o
        spot = peer if back else me
        return send(lists.at[rep, pl.ds(me, 1)] if k else skel, lists.at[rep, pl.ds(spot, 1)],
                    list_send.at[peer, rep], list_recv.at[spot, rep], peer, my_rep)

    def rows_x(o, back=False):
        return exchange(o, back, lambda p: rows_out.at[p, pl.ds(0, sent)], lambda p: rows_in.at[p, pl.ds(0, sent)], rows_send, rows_recv)

    def prod_x(o, back=False):
        return exchange(o, back, lambda p: prod_out.at[p, pl.ds(0, sent)], lambda p: prod_in.at[p, pl.ds(0, sent)], prod_send, prod_recv)

    def piece_x(k, back=False):
        rep = lax.rem(my_rep + k, reps)
        spot = rep if back else my_rep
        return send(skel, lists.at[spot, pl.ds(me, 1)], piece_send.at[rep], piece_recv.at[spot], me, rep)

    def side_x(o, back=False):
        spot = place[o] if back else place[-o]
        return send(omega, side.at[spot], side_send.at[place[o]], side_recv.at[spot], me + o, my_rep)

    barrier = pltpu.get_barrier_semaphore()
    for k in range(1, reps):
        signal(barrier, me, lax.rem(my_rep + k, reps))
    for o in close:
        if_there(o, lambda o=o: signal(barrier, me + o, my_rep))

    loads = [pltpu.make_async_copy(a, b, loaded.at[i]) for i, (a, b) in
             enumerate(((coords_in, coords), (omega_in, omega), (skel_in, skel)))]
    for load in loads:
        load.start()
    for load in loads:
        load.wait()
    own_points = coords[...]
    own_cols = jnp.transpose(jnp.concatenate([own_points, jnp.zeros((5, leaf), f32)], axis=0))
    points[me] = own_points
    lists[my_rep, pl.ds(me, 1)] = skel[...]
    rows_in[...] = jnp.zeros((n, cap, samp), bf16)
    prod_in[...] = jnp.zeros((n, cap, samp), bf16)

    edge = me * (n - 1 - me)
    for met, level in ((2, edge == 0), (3, edge == n - 2), (4, edge > n - 2)):
        @pl.when(level)
        def _():
            pl.semaphore_wait(barrier, reps - 1 + met)

    for k in range(1, reps):
        piece_x(k).start()
    for sign, sem in ((1, above), (-1, below)):
        def first(sign=sign, sem=sem):
            if_there(-2 * sign, lambda: signal(sem, me - 2 * sign, my_rep))
        if_there(sign, first)
    for o in close:
        if_there(o, lambda o=o: point_x(o).start())
    even = lax.rem(me, 2) == 0
    for o in (-2, 2):
        if_there(o, lambda o=o: side_x(o).start())
    for o in (-1, 1):
        @pl.when(even if o == 1 else jnp.logical_not(even))
        def _():
            if_there(o, lambda: side_x(o).start())
    for s in range(2, n // 2 + 1):
        for sign, sem in ((1, above), (-1, below)):
            def hop(s=s, sign=sign, sem=sem):
                pl.semaphore_wait(sem, 1)
                if_there(-2 * sign, lambda: signal(sem, me - 2 * sign, my_rep))
            if_there(sign * (2 * s - 1), hop)

    for k in range(1, reps):
        piece_x(k, True).wait_recv()
    for o in distant + list(close):
        def lists_out(o=o):
            for k in range(reps):
                list_x(o, k).start()
        if_there(o, lists_out)
    for o in distant:
        if_there(o, lambda o=o: point_x(o).start())
    for o in (-1, 1):
        @pl.when(even if o == -1 else jnp.logical_not(even))
        def _():
            if_there(o, lambda: side_x(o).start())
    total[...] = dot(tile(own_cols, own_points), omega[...])
    for o in distant + list(close):
        def lists_in(o=o):
            for k in range(reps):
                list_x(o, k, True).wait_recv()
        if_there(o, lists_in)

    listed = jnp.concatenate([lists[r] for r in range(reps)], axis=1)
    mine = jnp.concatenate([lists[r, pl.ds(me, 1)] for r in range(reps)], axis=1)
    local_own = lax.rem(listed, leaf).astype(f32)
    local_req = lax.rem(mine, leaf).astype(f32)
    hit_req = lax.div(mine, leaf) == lax.broadcasted_iota(jnp.int32, (n, rank), 0)
    hit_own = lax.div(listed, leaf) == me
    before = (lax.broadcasted_iota(jnp.int32, (rank, rank), 0)
              < lax.broadcasted_iota(jnp.int32, (rank, rank), 1)).astype(f32).astype(bf16)
    key_req = jnp.where(hit_req, dot(hit_req.astype(f32).astype(bf16), before), -1.0)
    key_own = jnp.where(hit_own, dot(hit_own.astype(f32).astype(bf16), before), -1.0)
    slot_ids = lax.broadcasted_iota(jnp.int32, (cap, rank), 0).astype(f32)
    leaf_ids = lax.broadcasted_iota(jnp.int32, (cap, leaf), 1).astype(f32)

    def picker(keys, local):
        found = jnp.sum(jnp.where(keys == slot_ids, local + 1.0, 0.0), axis=1, keepdims=True)
        return jnp.where(found - 1.0 == leaf_ids, 1.0, 0.0).astype(bf16)

    def places(pick, whole):
        high = whole.astype(bf16).astype(f32)
        middle = (whole - high).astype(bf16).astype(f32)
        low = whole - high - middle
        parts = jnp.concatenate([high, middle, low], axis=0).astype(bf16)
        got = lax.dot_general(pick, parts, (((1,), (1,)), ((), ())), preferred_element_type=f32)
        return got[:, 0:3] + got[:, 3:6] + got[:, 6:9]

    for i in range(n):
        pick = picker(key_own[i:i + 1], local_own[i:i + 1])
        pick_own[i] = pick
        rows_out[i] = dot(pick, omega[...]).astype(bf16)
    for o in distant:
        if_there(o, lambda o=o: rows_x(o).start())
    for o in distant + list(close):
        if_there(o, lambda o=o: point_x(o, True).wait_recv())
    for j in range(n):
        pick = picker(key_req[j:j + 1], local_req)
        pick_req[j] = pick
        skel_tile = tile(places(pick, points[j]), own_points)
        far_tile[j] = skel_tile
        prod_out[j] = dot(skel_tile, omega[...]).astype(bf16)
    for o in distant:
        if_there(o, lambda o=o: prod_x(o).start())

    def from_side(o):
        peer = me + o
        side_x(o, True).wait_recv()
        rows = side[place[o]]
        rows_in[peer] = dot(pick_req[peer], rows).astype(bf16)
        there = points[peer]
        prod_in[peer] = dot(tile(places(pick_own[peer], own_points), there), rows).astype(bf16)
        if abs(o) == 1:
            total[...] += dot(tile(own_cols, there), rows)

    for o in (-2, 2, -1, 1):
        if_there(o, lambda o=o: from_side(o))

    far = far_tile[...].reshape(n * cap, leaf).T
    back = pick_own[...].reshape(n * cap, leaf).T
    for o in distant:
        if_there(o, lambda o=o: rows_x(o, True).wait_recv())
    row_out[...] = total[...] + dot(far, rows_in[...].reshape(n * cap, samp))
    for o in distant:
        if_there(o, lambda o=o: prod_x(o, True).wait_recv())
    col_out[...] = dot(back, prod_in[...].reshape(n * cap, samp))

    for k in range(1, reps):
        piece_x(k).wait_send()
    for o in distant:
        def done(o=o):
            for x in (point_x, rows_x, prod_x):
                x(o).wait_send()
            for k in range(reps):
                list_x(o, k).wait_send()
        if_there(o, done)
    for o in close:
        def done(o=o):
            for x in (point_x, side_x):
                x(o).wait_send()
            for k in range(reps):
                list_x(o, k).wait_send()
        if_there(o, done)


def near_call(n, reps, cap, coords, omega, skeleton):
    leaf, samp = omega.shape
    piece = skeleton.shape[1]
    need = max(8, 2 * piece * reps // (n - 1))
    sent = need + need % 2
    vmem = pl.BlockSpec(memory_space=pltpu.VMEM)
    sem = pltpu.SemaphoreType.DMA
    return pl.pallas_call(
        functools.partial(near_kernel, n, reps, cap, sent),
        out_shape=(jax.ShapeDtypeStruct((leaf, samp), f32), jax.ShapeDtypeStruct((leaf, samp), f32)),
        in_specs=[pl.BlockSpec(memory_space=pl.ANY)] * 3,
        out_specs=(vmem, vmem),
        scratch_shapes=[
            pltpu.VMEM(coords.shape, f32),
            pltpu.VMEM(omega.shape, bf16),
            pltpu.VMEM(skeleton.shape, jnp.int32),
            pltpu.VMEM((reps, n, piece), jnp.int32),
            pltpu.VMEM((n, 3, leaf), f32),
            pltpu.VMEM((4, leaf, samp), bf16),
            pltpu.VMEM((n, cap, samp), bf16),
            pltpu.VMEM((n, cap, samp), bf16),
            pltpu.VMEM((n, cap, samp), bf16),
            pltpu.VMEM((n, cap, samp), bf16),
            pltpu.VMEM((n, cap, leaf), bf16),
            pltpu.VMEM((n, cap, leaf), bf16),
            pltpu.VMEM((n, cap, leaf), bf16),
            pltpu.VMEM((leaf, samp), f32),
            sem((3,)), sem((reps,)), sem((reps,)),
            sem((n, reps)), sem((n, reps)), sem((n,)), sem((n,)), sem((4,)), sem((4,)),
            sem((n,)), sem((n,)), sem((n,)), sem((n,)),
            pltpu.SemaphoreType.REGULAR, pltpu.SemaphoreType.REGULAR,
        ],
        compiler_params=pltpu.CompilerParams(collective_id=0, has_side_effects=True),
    )(coords, omega, skeleton)


def finish_kernel(row, col, row_out, col_out):
    row_out[...] = row[...].astype(bf16)
    col_out[...] = col[...]


def finish(row, col):
    vmem = pl.BlockSpec(memory_space=pltpu.VMEM)
    return pl.pallas_call(
        finish_kernel,
        out_shape=(jax.ShapeDtypeStruct(row.shape, bf16), jax.ShapeDtypeStruct(col.shape, f32)),
        in_specs=[vmem] * 2, out_specs=(vmem, vmem))(row, col)


def on_device(n, reps, coords, omega, skeleton):
    leaf, samp = omega.shape
    piece = skeleton.shape[1]
    rank = piece * reps
    cap = -(-max(8, 2 * rank // (n - 1)) // 16) * 16
    if 6 <= n <= 16:
        return finish(*near_call(n, reps, cap, coords, omega, skeleton))
    vmem = pl.BlockSpec(memory_space=pltpu.VMEM)
    sem = pltpu.SemaphoreType.DMA
    row, col = pl.pallas_call(
        functools.partial(kernel, n, reps, cap),
        out_shape=(jax.ShapeDtypeStruct((leaf, samp), f32), jax.ShapeDtypeStruct((leaf, samp), f32)),
        in_specs=[pl.BlockSpec(memory_space=pl.ANY)] * 3,
        out_specs=(vmem, vmem),
        scratch_shapes=[
            pltpu.VMEM(coords.shape, f32),
            pltpu.VMEM(omega.shape, bf16),
            pltpu.VMEM(skeleton.shape, jnp.int32),
            sem((3,)),
            pltpu.VMEM((reps, n, piece), jnp.int32),
            pltpu.VMEM((n, 3, leaf), f32),
            pltpu.VMEM((2, leaf, samp), bf16),
            pltpu.VMEM((2, n, rank), f32),
            pltpu.VMEM((1, rank), f32),
            pltpu.VMEM((n, rank), f32),
            pltpu.VMEM((n, cap, samp), bf16),
            pltpu.VMEM((n, cap, samp), bf16),
            pltpu.VMEM((n, cap, samp), bf16),
            pltpu.VMEM((n, cap, samp), bf16),
            pltpu.VMEM((n, cap, leaf), bf16),
            pltpu.VMEM((n, cap, leaf), bf16),
            pltpu.VMEM((leaf, samp), f32),
            sem((n * reps,)), sem((n * reps,)),
            sem((n,)), sem((n,)), sem((2,)), sem((2,)),
            sem((n,)), sem((n,)), sem((n,)), sem((n,)),
        ],
        compiler_params=pltpu.CompilerParams(collective_id=0, has_side_effects=True),
    )(coords, omega, skeleton)
    return finish(row, col)


def solution(mesh):
    in_specs = (P(None, "node"), P("node", "rep"), P("node", "rep"))
    out_specs = (P("node", "rep"), P("node", "rep"))
    body = functools.partial(on_device, mesh.shape["node"], mesh.shape["rep"])
    return jax.shard_map(body, mesh=mesh, in_specs=in_specs, out_specs=out_specs, check_vma=False)
```

profile of v0, /device:TPU:0, one launch (start us, length us, event | category | flops | bytes accessed | tf_op | source)
XLA Modules:
  0.0 24.8 jit_solution(14729968509680842786)
XLA Ops:
  0.6 22.4 %shard_map.50 = (f32[512,128]{1,0:T(8,128)}, f32[512,128]{1,0:T(8,128)}) custom-call(f32[3,512]{1,0:T(4,128)} %coords_in.1, bf16[512,128]{1,0:T(8,128)(2,1)} %omega_in.1, s32[1,64]{1,0:T(1,128)} %skel_in.1), custom_call_target="tpu_custom_call" | custom-call | tf_op jit(solution)/shard_map/pallas_call | solution.py:425
  23.0 1.8 %shard_map.51 = (bf16[512,128]{1,0:T(8,128)(2,1)}, f32[512,128]{1,0:T(8,128)}) custom-call(f32[512,128]{1,0:T(8,128)} %get-tuple-element.4.row, f32[512,128]{1,0:T(8,128)} %get-tuple-element.5.col), custom_call_target="tpu_custom_call" | custom-call | tf_op jit(solution)/shard_map/pallas_call | solution.py:461
where the time goes:
time: 25 us; the launch traced here: 24.8 us
  Pallas kernels  24.2 us (97%)
  between operations  0.64 us (3%)
    pallas_call x1, Pallas kernels, near_call(): pl.pallas_call(functools.partial(near_kernel, n, reps, cap, sent), out_sh...  22.4 us
    pallas_call x1, Pallas kernels, finish(): pl.pallas_call(finish_kernel, out_shape=(jax.ShapeDtypeStruct(row.shape,...  1.79 us

commit v1 on v0

--- a/solution.py
+++ b/solution.py
@@ -424,8 +424,8 @@
     sem = pltpu.SemaphoreType.DMA
     return pl.pallas_call(
         functools.partial(near_kernel, n, reps, cap, sent),
-        out_shape=(jax.ShapeDtypeStruct((leaf, samp), f32), jax.ShapeDtypeStruct((leaf, samp), f32)),
-        in_specs=[pl.BlockSpec(memory_space=pl.ANY)] * 3,
+        out_shape=(pltpu.VMEM((leaf, samp), f32), pltpu.VMEM((leaf, samp), f32)),
+        in_specs=[pl.BlockSpec(memory_space=pltpu.HBM)] * 3,
         out_specs=(vmem, vmem),
         scratch_shapes=[
             pltpu.VMEM(coords.shape, f32),
@@ -461,7 +461,8 @@
     return pl.pallas_call(
         finish_kernel,
         out_shape=(jax.ShapeDtypeStruct(row.shape, bf16), jax.ShapeDtypeStruct(col.shape, f32)),
-        in_specs=[vmem] * 2, out_specs=(vmem, vmem))(row, col)
+        in_specs=[vmem] * 2, out_specs=(vmem, vmem),
+        compiler_params=pltpu.CompilerParams(vmem_limit_bytes=16 << 20))(row, col)
 
 
 def on_device(n, reps, coords, omega, skeleton):

time: 25 us -> 23.2 us (0.928)
  Pallas kernels: 24.2 us -> 22.4 us
    pallas_call x1, Pallas kernels: 1.79 us -> 0.78 us  [finish(): pl.pallas_call(finish_kernel, out_shape=(jax.ShapeDtypeStruct(row.shape,...]
    pallas_call x1, Pallas kernels: 22.4 us -> 21.6 us  [near_call(): pl.pallas_call(functools.partial(near_kernel, n, reps, cap, sent), out_sh...]
where the time goes in v1:
time: 23.2 us; the launch traced here: 23 us
  Pallas kernels  22.4 us (97%)
  between operations  0.64 us (3%)
    pallas_call x1, Pallas kernels, near_call(): pl.pallas_call(functools.partial(near_kernel, n, reps, cap, sent), out_sh...  21.6 us
    pallas_call x1, Pallas kernels, finish(): pl.pallas_call(finish_kernel, out_shape=(jax.ShapeDtypeStruct(row.shape,...  0.78 us

profile of v1, /device:TPU:0, one launch (start us, length us, event | category | flops | bytes accessed | tf_op | source)
XLA Modules:
  0.0 23.0 jit_solution(4466748147979704643)
XLA Ops:
  0.6 21.6 %shard_map.50 = (f32[512,128]{1,0:T(8,128)S(1)}, f32[512,128]{1,0:T(8,128)S(1)}) custom-call(f32[3,512]{1,0:T(4,128)} %coords_in.1, bf16[512,128]{1,0:T(8,128)(2,1)} %omega_in.1, s32[1,64]{1,0:T(1,128)} %skel_in.1), custom_call_target="tpu_custom_call" | custom-call | tf_op jit(solution)/shard_map/pallas_call | solution.py:425
  22.2 0.8 %shard_map.51 = (bf16[512,128]{1,0:T(8,128)(2,1)}, f32[512,128]{1,0:T(8,128)}) custom-call(f32[512,128]{1,0:T(8,128)S(1)} %get-tuple-element.4.row, f32[512,128]{1,0:T(8,128)S(1)} %get-tuple-element.5.col), custom_call_target="tpu_custom_call" | custom-call | tf_op jit(solution)/shard_map/pallas_call | solution.py:461

commit v2 on v1

--- a/solution.py
+++ b/solution.py
@@ -30,11 +30,11 @@
         each(0, n - 1, lambda d: body(1 + lax.rem(d + half - 1, n - 1)))
 
 
-def tile(col, row):
+def tile(col, row, scale=kernel_scale):
     squared = (col[:, 0:1] - row[0:1, :]) ** 2
     squared = squared + (col[:, 1:2] - row[1:2, :]) ** 2
     squared = squared + (col[:, 2:3] - row[2:3, :]) ** 2
-    return (kernel_scale * lax.rsqrt(squared + softening * softening)).astype(bf16)
+    return (scale * lax.rsqrt(squared + softening * softening)).astype(bf16)
 
 
 def dot(a, b):
@@ -213,16 +213,30 @@
 
 
 def near_kernel(n, reps, cap, sent, coords_in, omega_in, skel_in, row_out, col_out,
-                coords, omega, skel, lists, points, side, rows_out, rows_in, prod_out,
-                prod_in, pick_own, pick_req, far_tile, total,
-                loaded, piece_send, piece_recv, list_send, list_recv, point_send, point_recv,
-                side_send, side_recv, rows_send, rows_recv, prod_send, prod_recv, above, below):
+                coords, omega, skel, pieces, code_out, code_in, points, side, rows_out, rows_in, prod_out,
+                prod_in, pick_own, pick_req, far_tile, near_tile, edge_tile, edge_prod, total,
+                loaded, piece_send, piece_recv, point_send, point_recv, code_send, code_recv,
+                side_send, side_recv, rows_send, rows_recv, prod_send, prod_recv, ready):
     leaf, samp = omega.shape
     rank = skel.shape[1] * reps
     me, my_rep = lax.axis_index("node"), lax.axis_index("rep")
-    close = (-2, -1, 1, 2)
-    distant = [o * sign for o in sorted(range(3, n), key=lambda o: abs(o - n // 2)) for sign in (1, -1)]
-    place = {o: k for k, o in enumerate(close)}
+    first, last = (n - me) // n, (me + 1) // n
+    edge = first + last
+    beside = (1, -1)
+    parts, slots = side_send.shape[1], n - 2
+    late = range(3, n)
+
+    def peer_of(k):
+        before_me = (me + n - k - 2) // n
+        return before_me * k + (1 - before_me) * (3 + k - first)
+
+    peers = [peer_of(k) for k in range(n - 3)]
+    peers.append(edge * peer_of(n - 3) + (1 - edge) * me)
+
+    def if_edge(body):
+        @pl.when(edge == 1)
+        def _():
+            body()
 
     def if_there(offset, body):
         @pl.when(me + offset < n if offset > 0 else me + offset >= 0)
@@ -237,117 +251,102 @@
             src_ref=src, dst_ref=dst, send_sem=send_sem, recv_sem=recv_sem,
             device_id={"node": node, "rep": rep}, device_id_type=MESH)
 
-    def exchange(offset, back, src, dst, send_sems, recv_sems):
-        peer = me + offset
+    def exchange(peer, back, src, dst, send_sems, recv_sems):
         spot = peer if back else me
         return send(src(peer), dst(spot), send_sems.at[peer], recv_sems.at[spot], peer, my_rep)
 
-    def point_x(o, back=False):
-        return exchange(o, back, lambda p: coords, lambda p: points.at[p], point_send, point_recv)
-
-    def list_x(o, k, back=False):
-        rep, peer = lax.rem(my_rep + k, reps), me + o
-        spot = peer if back else me
-        return send(lists.at[rep, pl.ds(me, 1)] if k else skel, lists.at[rep, pl.ds(spot, 1)],
-                    list_send.at[peer, rep], list_recv.at[spot, rep], peer, my_rep)
-
-    def rows_x(o, back=False):
-        return exchange(o, back, lambda p: rows_out.at[p, pl.ds(0, sent)], lambda p: rows_in.at[p, pl.ds(0, sent)], rows_send, rows_recv)
-
-    def prod_x(o, back=False):
-        return exchange(o, back, lambda p: prod_out.at[p, pl.ds(0, sent)], lambda p: prod_in.at[p, pl.ds(0, sent)], prod_send, prod_recv)
+    def point_x(peer, back=False):
+        return exchange(peer, back, lambda p: coords, lambda p: points.at[p], point_send, point_recv)
+
+    def code_x(peer, back=False):
+        return exchange(peer, back, lambda p: code_out.at[p], lambda p: code_in.at[p], code_send, code_recv)
+
+    def rows_x(peer, back=False):
+        return exchange(peer, back, lambda p: rows_out.at[p, pl.ds(0, sent)], lambda p: rows_in.at[p, pl.ds(0, sent)], rows_send, rows_recv)
+
+    def prod_x(peer, back=False):
+        return exchange(peer, back, lambda p: prod_out.at[p, pl.ds(0, sent)], lambda p: prod_in.at[p, pl.ds(0, sent)], prod_send, prod_recv)
+
+    def side_x(slot, part, back=False):
+        spot = slot if back else 1 - slot
+        rows = pl.ds(part * (leaf // parts), leaf // parts)
+        return send(omega.at[rows], side.at[spot, rows], side_send.at[slot, part], side_recv.at[spot, part], me + beside[slot], my_rep)
 
     def piece_x(k, back=False):
         rep = lax.rem(my_rep + k, reps)
         spot = rep if back else my_rep
-        return send(skel, lists.at[spot, pl.ds(me, 1)], piece_send.at[rep], piece_recv.at[spot], me, rep)
-
-    def side_x(o, back=False):
-        spot = place[o] if back else place[-o]
-        return send(omega, side.at[spot], side_send.at[place[o]], side_recv.at[spot], me + o, my_rep)
+        return send(skel, pieces.at[spot], piece_send.at[rep], piece_recv.at[spot], me, rep)
 
     barrier = pltpu.get_barrier_semaphore()
     for k in range(1, reps):
         signal(barrier, me, lax.rem(my_rep + k, reps))
-    for o in close:
+    for o in (-1, -2, *range(1, n)):
         if_there(o, lambda o=o: signal(barrier, me + o, my_rep))
 
     loads = [pltpu.make_async_copy(a, b, loaded.at[i]) for i, (a, b) in
-             enumerate(((coords_in, coords), (omega_in, omega), (skel_in, skel)))]
+             enumerate(((skel_in, skel), (coords_in, coords), (omega_in, omega)))]
     for load in loads:
         load.start()
     for load in loads:
         load.wait()
     own_points = coords[...]
     own_cols = jnp.transpose(jnp.concatenate([own_points, jnp.zeros((5, leaf), f32)], axis=0))
-    points[me] = own_points
-    lists[my_rep, pl.ds(me, 1)] = skel[...]
+    pieces[my_rep] = skel[...]
     rows_in[...] = jnp.zeros((n, cap, samp), bf16)
     prod_in[...] = jnp.zeros((n, cap, samp), bf16)
-
-    edge = me * (n - 1 - me)
-    for met, level in ((2, edge == 0), (3, edge == n - 2), (4, edge > n - 2)):
-        @pl.when(level)
-        def _():
-            pl.semaphore_wait(barrier, reps - 1 + met)
+    edge_prod[...] = jnp.zeros((2, cap, samp), bf16)
+    far_tile[slots - 1] = jnp.zeros((cap, leaf), bf16)
+    for k in range(slots - 1, n):
+        pick_own[k] = jnp.zeros((cap, leaf), bf16)
+
+    def push(part):
+        for slot in (0, 1):
+            if_there(beside[slot], lambda slot=slot: side_x(slot, part).start())
+
+    with jax.named_scope("enter"):
+        pl.semaphore_wait(barrier, reps + 1 + me - last - (me + 2) // n)
 
     for k in range(1, reps):
         piece_x(k).start()
-    for sign, sem in ((1, above), (-1, below)):
-        def first(sign=sign, sem=sem):
-            if_there(-2 * sign, lambda: signal(sem, me - 2 * sign, my_rep))
-        if_there(sign, first)
-    for o in close:
-        if_there(o, lambda o=o: point_x(o).start())
-    even = lax.rem(me, 2) == 0
-    for o in (-2, 2):
-        if_there(o, lambda o=o: side_x(o).start())
-    for o in (-1, 1):
-        @pl.when(even if o == 1 else jnp.logical_not(even))
-        def _():
-            if_there(o, lambda: side_x(o).start())
-    for s in range(2, n // 2 + 1):
-        for sign, sem in ((1, above), (-1, below)):
-            def hop(s=s, sign=sign, sem=sem):
-                pl.semaphore_wait(sem, 1)
-                if_there(-2 * sign, lambda: signal(sem, me - 2 * sign, my_rep))
-            if_there(sign * (2 * s - 1), hop)
-
-    for k in range(1, reps):
-        piece_x(k, True).wait_recv()
-    for o in distant + list(close):
-        def lists_out(o=o):
-            for k in range(reps):
-                list_x(o, k).start()
-        if_there(o, lists_out)
-    for o in distant:
-        if_there(o, lambda o=o: point_x(o).start())
-    for o in (-1, 1):
-        @pl.when(even if o == -1 else jnp.logical_not(even))
-        def _():
-            if_there(o, lambda: side_x(o).start())
-    total[...] = dot(tile(own_cols, own_points), omega[...])
-    for o in distant + list(close):
-        def lists_in(o=o):
-            for k in range(reps):
-                list_x(o, k, True).wait_recv()
-        if_there(o, lists_in)
-
-    listed = jnp.concatenate([lists[r] for r in range(reps)], axis=1)
-    mine = jnp.concatenate([lists[r, pl.ds(me, 1)] for r in range(reps)], axis=1)
-    local_own = lax.rem(listed, leaf).astype(f32)
-    local_req = lax.rem(mine, leaf).astype(f32)
-    hit_req = lax.div(mine, leaf) == lax.broadcasted_iota(jnp.int32, (n, rank), 0)
-    hit_own = lax.div(listed, leaf) == me
+    for o in late:
+        if_there(-o, lambda o=o: signal(ready.at[me], me - o, my_rep))
+    known = (1, 2, *range(-1, -n, -1))
+    for o in known:
+        if_there(o, lambda o=o: point_x(me + o).start())
+    push(0)
+
+    with jax.named_scope("own"):
+        total[...] = dot(tile(own_cols, own_points), omega[...])
+
+    with jax.named_scope("pieces"):
+        for k in range(1, reps):
+            piece_x(k, True).wait_recv()
+    mine = jnp.concatenate([pieces[r] for r in range(reps)], axis=1)
+    local = lax.rem(mine, leaf).astype(f32)
     before = (lax.broadcasted_iota(jnp.int32, (rank, rank), 0)
               < lax.broadcasted_iota(jnp.int32, (rank, rank), 1)).astype(f32).astype(bf16)
-    key_req = jnp.where(hit_req, dot(hit_req.astype(f32).astype(bf16), before), -1.0)
-    key_own = jnp.where(hit_own, dot(hit_own.astype(f32).astype(bf16), before), -1.0)
+    hit = lax.div(mine, leaf) == lax.broadcasted_iota(jnp.int32, (n, rank), 0)
+    keys = jnp.where(hit, dot(hit.astype(f32).astype(bf16), before), -1.0)
+    codes = jnp.where(hit, (keys + 1.0) * leaf + local, 0.0).astype(jnp.int32)
+    for i in range(n):
+        code_out[i] = codes[i:i + 1]
+    for o in known:
+        if_there(o, lambda o=o: code_x(me + o).start())
+
+    for o in late:
+        def follow(o=o):
+            with jax.named_scope(f"ready{o}"):
+                pl.semaphore_wait(ready.at[me + o], 1)
+            point_x(me + o).start()
+            code_x(me + o).start()
+        if_there(o, follow)
+    push(1)
+
     slot_ids = lax.broadcasted_iota(jnp.int32, (cap, rank), 0).astype(f32)
     leaf_ids = lax.broadcasted_iota(jnp.int32, (cap, leaf), 1).astype(f32)
 
-    def picker(keys, local):
-        found = jnp.sum(jnp.where(keys == slot_ids, local + 1.0, 0.0), axis=1, keepdims=True)
+    def picker(key, index):
+        found = jnp.sum(jnp.where(key == slot_ids, index + 1.0, 0.0), axis=1, keepdims=True)
         return jnp.where(found - 1.0 == leaf_ids, 1.0, 0.0).astype(bf16)
 
     def places(pick, whole):
@@ -358,61 +357,106 @@
         got = lax.dot_general(pick, parts, (((1,), (1,)), ((), ())), preferred_element_type=f32)
         return got[:, 0:3] + got[:, 3:6] + got[:, 6:9]
 
-    for i in range(n):
-        pick = picker(key_own[i:i + 1], local_own[i:i + 1])
-        pick_own[i] = pick
-        rows_out[i] = dot(pick, omega[...]).astype(bf16)
-    for o in distant:
-        if_there(o, lambda o=o: rows_x(o).start())
-    for o in distant + list(close):
-        if_there(o, lambda o=o: point_x(o, True).wait_recv())
-    for j in range(n):
-        pick = picker(key_req[j:j + 1], local_req)
-        pick_req[j] = pick
-        skel_tile = tile(places(pick, points[j]), own_points)
-        far_tile[j] = skel_tile
-        prod_out[j] = dot(skel_tile, omega[...]).astype(bf16)
-    for o in distant:
-        if_there(o, lambda o=o: prod_x(o).start())
-
-    def from_side(o):
-        peer = me + o
-        side_x(o, True).wait_recv()
-        rows = side[place[o]]
-        rows_in[peer] = dot(pick_req[peer], rows).astype(bf16)
-        there = points[peer]
-        prod_in[peer] = dot(tile(places(pick_own[peer], own_points), there), rows).astype(bf16)
-        if abs(o) == 1:
-            total[...] += dot(tile(own_cols, there), rows)
-
-    for o in (-2, 2, -1, 1):
-        if_there(o, lambda o=o: from_side(o))
-
-    far = far_tile[...].reshape(n * cap, leaf).T
-    back = pick_own[...].reshape(n * cap, leaf).T
-    for o in distant:
-        if_there(o, lambda o=o: rows_x(o, True).wait_recv())
-    row_out[...] = total[...] + dot(far, rows_in[...].reshape(n * cap, samp))
-    for o in distant:
-        if_there(o, lambda o=o: prod_x(o, True).wait_recv())
-    col_out[...] = dot(back, prod_in[...].reshape(n * cap, samp))
-
-    for k in range(1, reps):
-        piece_x(k).wait_send()
-    for o in distant:
-        def done(o=o):
-            for x in (point_x, rows_x, prod_x):
-                x(o).wait_send()
-            for k in range(reps):
-                list_x(o, k).wait_send()
-        if_there(o, done)
-    for o in close:
-        def done(o=o):
-            for x in (point_x, side_x):
-                x(o).wait_send()
-            for k in range(reps):
-                list_x(o, k).wait_send()
-        if_there(o, done)
+    def asked(peer):
+        code = code_in[peer]
+        return picker((lax.div(code, leaf) - 1).astype(f32), lax.rem(code, leaf).astype(f32))
+
+    with jax.named_scope("requests"):
+        for i in range(n):
+            pick_req[i] = picker(keys[i:i + 1], local)
+
+    def serve(group):
+        with jax.named_scope("wait" + "".join(map(str, group))):
+            for k in group:
+                point_x(peers[k], True).wait_recv()
+                code_x(peers[k], True).wait_recv()
+        with jax.named_scope("serve" + "".join(map(str, group))):
+            picks = [asked(peers[k]) for k in group]
+            tiles = [tile(places(pick_req[peers[k]], points[peers[k]]), own_points) for k in group]
+            for k, pick in zip(group, picks):
+                pick_own[k] = pick
+                rows_out[peers[k]] = dot(pick, omega[...]).astype(bf16)
+            for k, skel_tile in zip(group, tiles):
+                far_tile[k] = skel_tile
+                prod_out[peers[k]] = dot(skel_tile, omega[...]).astype(bf16)
+        for k in group:
+            rows_x(peers[k]).start()
+            prod_x(peers[k]).start()
+
+    for k in range(0, n - 3, 2):
+        serve(list(range(k, min(k + 2, n - 3))))
+    if_edge(lambda: serve([n - 3]))
+
+    def prepare(slot):
+        peer = me + beside[slot]
+        with jax.named_scope(f"besidewait{slot}"):
+            point_x(peer, True).wait_recv()
+            code_x(peer, True).wait_recv()
+        with jax.named_scope(f"beside{slot}"):
+            there = points[peer]
+            counted = jnp.sum(pick_req[peer].astype(f32), axis=0, keepdims=True) + 1.0
+            near_tile[slot] = tile(own_cols, there, kernel_scale * counted)
+            pick = asked(peer)
+            pick_own[slots + slot] = pick
+            edge_tile[slot] = tile(places(pick, own_points), there)
+
+    def collect(slot):
+        with jax.named_scope(f"side{slot}"):
+            for part in range(parts):
+                side_x(slot, part, True).wait_recv()
+        with jax.named_scope(f"near{slot}"):
+            edge_prod[slot] = dot(edge_tile[slot], side[slot]).astype(bf16)
+            total[...] += dot(near_tile[slot], side[slot])
+
+    for slot in (0, 1):
+        if_there(beside[slot], lambda slot=slot: prepare(slot))
+
+    with jax.named_scope("turn"):
+        far = far_tile[...].reshape(slots * cap, leaf).T
+        back = pick_own[...].reshape(n * cap, leaf).T
+
+    with jax.named_scope("sent"):
+        for k in range(1, reps):
+            piece_x(k).wait_send()
+        for o in range(1, n):
+            peer = lax.rem(me + o, n)
+            point_x(peer).wait_send()
+            code_x(peer).wait_send()
+
+    for slot in (0, 1):
+        if_there(beside[slot], lambda slot=slot: collect(slot))
+
+    def gather(x, name):
+        for k in range(n - 3):
+            with jax.named_scope(f"{name}{k}"):
+                x(peers[k], True).wait_recv()
+
+        def more():
+            with jax.named_scope(f"{name}{n - 3}"):
+                x(peers[n - 3], True).wait_recv()
+        if_edge(more)
+
+    gather(rows_x, "rows")
+    with jax.named_scope("rowsum"):
+        row_out[...] = total[...] + dot(far, jnp.concatenate([rows_in[p] for p in peers], axis=0))
+    gather(prod_x, "prod")
+    with jax.named_scope("colsum"):
+        col_out[...] = dot(back, jnp.concatenate([prod_in[p] for p in peers] + [edge_prod[0], edge_prod[1]], axis=0))
+
+    with jax.named_scope("sent2"):
+        for slot in (0, 1):
+            def sent_side(slot=slot):
+                for part in range(parts):
+                    side_x(slot, part).wait_send()
+            if_there(beside[slot], sent_side)
+        for peer in peers[:-1]:
+            rows_x(peer).wait_send()
+            prod_x(peer).wait_send()
+
+        def rest():
+            rows_x(peers[-1]).wait_send()
+            prod_x(peers[-1]).wait_send()
+        if_edge(rest)
 
 
 def near_call(n, reps, cap, coords, omega, skeleton):
@@ -431,21 +475,26 @@
             pltpu.VMEM(coords.shape, f32),
             pltpu.VMEM(omega.shape, bf16),
             pltpu.VMEM(skeleton.shape, jnp.int32),
-            pltpu.VMEM((reps, n, piece), jnp.int32),
+            pltpu.VMEM((reps, 1, piece), jnp.int32),
+            pltpu.VMEM((n, 1, piece * reps), jnp.int32),
+            pltpu.VMEM((n, 1, piece * reps), jnp.int32),
             pltpu.VMEM((n, 3, leaf), f32),
-            pltpu.VMEM((4, leaf, samp), bf16),
+            pltpu.VMEM((2, leaf, samp), bf16),
             pltpu.VMEM((n, cap, samp), bf16),
             pltpu.VMEM((n, cap, samp), bf16),
             pltpu.VMEM((n, cap, samp), bf16),
             pltpu.VMEM((n, cap, samp), bf16),
             pltpu.VMEM((n, cap, leaf), bf16),
             pltpu.VMEM((n, cap, leaf), bf16),
-            pltpu.VMEM((n, cap, leaf), bf16),
+            pltpu.VMEM((n - 2, cap, leaf), bf16),
+            pltpu.VMEM((2, leaf, leaf), bf16),
+            pltpu.VMEM((2, cap, leaf), bf16),
+            pltpu.VMEM((2, cap, samp), bf16),
             pltpu.VMEM((leaf, samp), f32),
             sem((3,)), sem((reps,)), sem((reps,)),
-            sem((n, reps)), sem((n, reps)), sem((n,)), sem((n,)), sem((4,)), sem((4,)),
+            sem((n,)), sem((n,)), sem((n,)), sem((n,)), sem((2, 2)), sem((2, 2)),
             sem((n,)), sem((n,)), sem((n,)), sem((n,)),
-            pltpu.SemaphoreType.REGULAR, pltpu.SemaphoreType.REGULAR,
+            pltpu.SemaphoreType.REGULAR((n,)),
         ],
         compiler_params=pltpu.CompilerParams(collective_id=0, has_side_effects=True),
     )(coords, omega, skeleton)

time: 23.2 us -> 20 us (0.86)
  Pallas kernels: 22.4 us -> 19.2 us
    pallas_call x1, Pallas kernels: 21.6 us -> 18.4 us  [near_call(): pl.pallas_call(functools.partial(near_kernel, n, reps, cap, sent), out_sh...]
where the time goes in v2:
time: 20 us; the launch traced here: 19.8 us
  Pallas kernels  19.2 us (96%)
  between operations  0.64 us (3%)
    pallas_call x1, Pallas kernels, near_call(): pl.pallas_call(functools.partial(near_kernel, n, reps, cap, sent), out_sh...  18.4 us
    pallas_call x1, Pallas kernels, finish(): pl.pallas_call(finish_kernel, out_shape=(jax.ShapeDtypeStruct(row.shape,...  0.78 us

profile of v2, /device:TPU:0, one launch (start us, length us, event | category | flops | bytes accessed | tf_op | source)
XLA Modules:
  0.0 19.8 jit_solution(10701866210797703762)
XLA Ops:
  0.6 18.4 %shard_map.50 = (f32[512,128]{1,0:T(8,128)S(1)}, f32[512,128]{1,0:T(8,128)S(1)}) custom-call(f32[3,512]{1,0:T(4,128)} %coords_in.1, bf16[512,128]{1,0:T(8,128)(2,1)} %omega_in.1, s32[1,64]{1,0:T(1,128)} %skel_in.1), custom_call_target="tpu_custom_call" | custom-call | tf_op jit(solution)/shard_map/pallas_call | solution.py:469
  19.0 0.8 %shard_map.51 = (bf16[512,128]{1,0:T(8,128)(2,1)}, f32[512,128]{1,0:T(8,128)}) custom-call(f32[512,128]{1,0:T(8,128)S(1)} %get-tuple-element.4.row, f32[512,128]{1,0:T(8,128)S(1)} %get-tuple-element.5.col), custom_call_target="tpu_custom_call" | custom-call | tf_op jit(solution)/shard_map/pallas_call | solution.py:510

commit v3 on v2

--- a/solution.py
+++ b/solution.py
@@ -215,15 +215,15 @@
 def near_kernel(n, reps, cap, sent, coords_in, omega_in, skel_in, row_out, col_out,
                 coords, omega, skel, pieces, code_out, code_in, points, side, rows_out, rows_in, prod_out,
                 prod_in, pick_own, pick_req, far_tile, near_tile, edge_tile, edge_prod, total,
-                loaded, piece_send, piece_recv, point_send, point_recv, code_send, code_recv,
-                side_send, side_recv, rows_send, rows_recv, prod_send, prod_recv, ready):
+                loaded, piece_send, piece_recv, point_send, code_send, point_recv, code_recv,
+                side_send, side_recv, rows_send, rows_recv, prod_send, prod_recv, ready, mates):
     leaf, samp = omega.shape
     rank = skel.shape[1] * reps
     me, my_rep = lax.axis_index("node"), lax.axis_index("rep")
     first, last = (n - me) // n, (me + 1) // n
     edge = first + last
     beside = (1, -1)
-    parts, slots = side_send.shape[1], n - 2
+    parts, slots = 2, n - 2
     late = range(3, n)
 
     def peer_of(k):
@@ -251,44 +251,69 @@
             src_ref=src, dst_ref=dst, send_sem=send_sem, recv_sem=recv_sem,
             device_id={"node": node, "rep": rep}, device_id_type=MESH)
 
-    def exchange(peer, back, src, dst, send_sems, recv_sems):
-        spot = peer if back else me
-        return send(src(peer), dst(spot), send_sems.at[peer], recv_sems.at[spot], peer, my_rep)
-
-    def point_x(peer, back=False):
-        return exchange(peer, back, lambda p: coords, lambda p: points.at[p], point_send, point_recv)
-
-    def code_x(peer, back=False):
-        return exchange(peer, back, lambda p: code_out.at[p], lambda p: code_in.at[p], code_send, code_recv)
-
-    def rows_x(peer, back=False):
-        return exchange(peer, back, lambda p: rows_out.at[p, pl.ds(0, sent)], lambda p: rows_in.at[p, pl.ds(0, sent)], rows_send, rows_recv)
-
-    def prod_x(peer, back=False):
-        return exchange(peer, back, lambda p: prod_out.at[p, pl.ds(0, sent)], lambda p: prod_in.at[p, pl.ds(0, sent)], prod_send, prod_recv)
-
-    def side_x(slot, part, back=False):
-        spot = slot if back else 1 - slot
+    def wait(like, sem):
+        pltpu.make_async_copy(like, like, sem).wait()
+
+    def point_x(peer):
+        return send(coords, points.at[me], point_send, point_recv.at[me], peer, my_rep)
+
+    def code_x(peer):
+        return send(code_out.at[peer], code_in.at[me], code_send, code_recv.at[me], peer, my_rep)
+
+    def hinted(peer):
+        wait(coords, point_recv.at[peer])
+        wait(code_out.at[0], code_recv.at[peer])
+
+    def rows_x(peer):
+        return send(rows_out.at[peer, pl.ds(0, sent)], rows_in.at[me, pl.ds(0, sent)], rows_send, rows_recv, peer, my_rep)
+
+    def prod_x(peer):
+        return send(prod_out.at[peer, pl.ds(0, sent)], prod_in.at[me, pl.ds(0, sent)], prod_send, prod_recv, peer, my_rep)
+
+    def push(slot, part):
         rows = pl.ds(part * (leaf // parts), leaf // parts)
-        return send(omega.at[rows], side.at[spot, rows], side_send.at[slot, part], side_recv.at[spot, part], me + beside[slot], my_rep)
-
-    def piece_x(k, back=False):
-        rep = lax.rem(my_rep + k, reps)
-        spot = rep if back else my_rep
-        return send(skel, pieces.at[spot], piece_send.at[rep], piece_recv.at[spot], me, rep)
-
-    barrier = pltpu.get_barrier_semaphore()
-    for k in range(1, reps):
-        signal(barrier, me, lax.rem(my_rep + k, reps))
-    for o in (-1, -2, *range(1, n)):
-        if_there(o, lambda o=o: signal(barrier, me + o, my_rep))
+        send(omega.at[rows], side.at[1 - slot, rows], side_send.at[slot], side_recv.at[1 - slot], me + beside[slot], my_rep).start()
+
+    def piece_x(rep):
+        return send(skel, pieces.at[my_rep], piece_send, piece_recv, me, rep)
 
     loads = [pltpu.make_async_copy(a, b, loaded.at[i]) for i, (a, b) in
              enumerate(((skel_in, skel), (coords_in, coords), (omega_in, omega)))]
     for load in loads:
         load.start()
-    for load in loads:
-        load.wait()
+
+    barrier = pltpu.get_barrier_semaphore()
+    for o in range(1, n):
+        if_there(o, lambda o=o: signal(barrier, me + o, my_rep))
+    for r in range(1, reps):
+        @pl.when(my_rep < r)
+        def _():
+            signal(barrier, me, r)
+
+    with jax.named_scope("enter"):
+        @pl.when(me + my_rep > 0)
+        def _():
+            pl.semaphore_wait(barrier, me + my_rep)
+
+    for r in range(reps - 1):
+        @pl.when(my_rep > r)
+        def _():
+            signal(mates, me, r)
+    for o in range(1, n):
+        if_there(-o, lambda o=o: signal(ready.at[me], me - o, my_rep))
+
+    with jax.named_scope("load"):
+        loads[0].wait()
+    for r in range(reps - 1):
+        @pl.when(my_rep > r)
+        def _():
+            piece_x(r).start()
+    loads[1].wait()
+    for o in range(1, n):
+        if_there(-o, lambda o=o: point_x(me - o).start())
+    loads[2].wait()
+    if_there(-1, lambda: push(1, 0))
+
     own_points = coords[...]
     own_cols = jnp.transpose(jnp.concatenate([own_points, jnp.zeros((5, leaf), f32)], axis=0))
     pieces[my_rep] = skel[...]
@@ -299,28 +324,30 @@
     for k in range(slots - 1, n):
         pick_own[k] = jnp.zeros((cap, leaf), bf16)
 
-    def push(part):
-        for slot in (0, 1):
-            if_there(beside[slot], lambda slot=slot: side_x(slot, part).start())
-
-    with jax.named_scope("enter"):
-        pl.semaphore_wait(barrier, reps + 1 + me - last - (me + 2) // n)
-
-    for k in range(1, reps):
-        piece_x(k).start()
-    for o in late:
-        if_there(-o, lambda o=o: signal(ready.at[me], me - o, my_rep))
-    known = (1, 2, *range(-1, -n, -1))
-    for o in known:
-        if_there(o, lambda o=o: point_x(me + o).start())
-    push(0)
-
     with jax.named_scope("own"):
         total[...] = dot(tile(own_cols, own_points), omega[...])
 
+    with jax.named_scope("mates"):
+        @pl.when(my_rep < reps - 1)
+        def _():
+            pl.semaphore_wait(mates, reps - 1 - my_rep)
+    for r in range(1, reps):
+        @pl.when(my_rep < r)
+        def _():
+            piece_x(r).start()
+
+    def meet(o):
+        with jax.named_scope(f"ready{o}"):
+            pl.semaphore_wait(ready.at[me + o], 1)
+        point_x(me + o).start()
+        if o == 1:
+            push(0, 0)
+
+    for o in (1, 2):
+        if_there(o, lambda o=o: meet(o))
+
     with jax.named_scope("pieces"):
-        for k in range(1, reps):
-            piece_x(k, True).wait_recv()
+        wait(pieces.at[pl.ds(0, reps - 1)], piece_recv)
     mine = jnp.concatenate([pieces[r] for r in range(reps)], axis=1)
     local = lax.rem(mine, leaf).astype(f32)
     before = (lax.broadcasted_iota(jnp.int32, (rank, rank), 0)
@@ -330,17 +357,15 @@
     codes = jnp.where(hit, (keys + 1.0) * leaf + local, 0.0).astype(jnp.int32)
     for i in range(n):
         code_out[i] = codes[i:i + 1]
-    for o in known:
+    for o in (*range(-n + 1, 0), 1, 2):
         if_there(o, lambda o=o: code_x(me + o).start())
-
-    for o in late:
+    for o in range(3, n):
         def follow(o=o):
-            with jax.named_scope(f"ready{o}"):
-                pl.semaphore_wait(ready.at[me + o], 1)
-            point_x(me + o).start()
+            meet(o)
             code_x(me + o).start()
         if_there(o, follow)
-    push(1)
+    for slot in (0, 1):
+        if_there(beside[slot], lambda slot=slot: push(slot, 1))
 
     slot_ids = lax.broadcasted_iota(jnp.int32, (cap, rank), 0).astype(f32)
     leaf_ids = lax.broadcasted_iota(jnp.int32, (cap, leaf), 1).astype(f32)
@@ -368,8 +393,7 @@
     def serve(group):
         with jax.named_scope("wait" + "".join(map(str, group))):
             for k in group:
-                point_x(peers[k], True).wait_recv()
-                code_x(peers[k], True).wait_recv()
+                hinted(peers[k])
         with jax.named_scope("serve" + "".join(map(str, group))):
             picks = [asked(peers[k]) for k in group]
             tiles = [tile(places(pick_req[peers[k]], points[peers[k]]), own_points) for k in group]
@@ -383,15 +407,14 @@
             rows_x(peers[k]).start()
             prod_x(peers[k]).start()
 
-    for k in range(0, n - 3, 2):
-        serve(list(range(k, min(k + 2, n - 3))))
+    for group in ([0], *([k, k + 1] for k in range(1, n - 4, 2)), *([[n - 4]] if n % 2 else [])):
+        serve(group)
     if_edge(lambda: serve([n - 3]))
 
     def prepare(slot):
         peer = me + beside[slot]
         with jax.named_scope(f"besidewait{slot}"):
-            point_x(peer, True).wait_recv()
-            code_x(peer, True).wait_recv()
+            hinted(peer)
         with jax.named_scope(f"beside{slot}"):
             there = points[peer]
             counted = jnp.sum(pick_req[peer].astype(f32), axis=0, keepdims=True) + 1.0
@@ -402,8 +425,7 @@
 
     def collect(slot):
         with jax.named_scope(f"side{slot}"):
-            for part in range(parts):
-                side_x(slot, part, True).wait_recv()
+            wait(side.at[slot], side_recv.at[slot])
         with jax.named_scope(f"near{slot}"):
             edge_prod[slot] = dot(edge_tile[slot], side[slot]).astype(bf16)
             total[...] += dot(near_tile[slot], side[slot])
@@ -416,47 +438,39 @@
         back = pick_own[...].reshape(n * cap, leaf).T
 
     with jax.named_scope("sent"):
-        for k in range(1, reps):
-            piece_x(k).wait_send()
-        for o in range(1, n):
-            peer = lax.rem(me + o, n)
-            point_x(peer).wait_send()
-            code_x(peer).wait_send()
+        wait(pieces.at[pl.ds(0, reps - 1)], piece_send)
+        wait(points.at[pl.ds(0, n - 1)], point_send)
+        wait(code_out.at[pl.ds(0, n - 1)], code_send)
 
     for slot in (0, 1):
         if_there(beside[slot], lambda slot=slot: collect(slot))
 
-    def gather(x, name):
-        for k in range(n - 3):
-            with jax.named_scope(f"{name}{k}"):
-                x(peers[k], True).wait_recv()
-
-        def more():
-            with jax.named_scope(f"{name}{n - 3}"):
-                x(peers[n - 3], True).wait_recv()
-        if_edge(more)
-
-    gather(rows_x, "rows")
+    def gather(like, sem):
+        def some(count):
+            wait(like.at[pl.ds(0, count), pl.ds(0, sent)], sem)
+
+        @pl.when(edge == 1)
+        def _():
+            some(n - 2)
+
+        @pl.when(edge == 0)
+        def _():
+            some(n - 3)
+
+    with jax.named_scope("rows"):
+        gather(rows_in, rows_recv)
     with jax.named_scope("rowsum"):
         row_out[...] = total[...] + dot(far, jnp.concatenate([rows_in[p] for p in peers], axis=0))
-    gather(prod_x, "prod")
+    with jax.named_scope("prods"):
+        gather(prod_in, prod_recv)
     with jax.named_scope("colsum"):
         col_out[...] = dot(back, jnp.concatenate([prod_in[p] for p in peers] + [edge_prod[0], edge_prod[1]], axis=0))
 
     with jax.named_scope("sent2"):
         for slot in (0, 1):
-            def sent_side(slot=slot):
-                for part in range(parts):
-                    side_x(slot, part).wait_send()
-            if_there(beside[slot], sent_side)
-        for peer in peers[:-1]:
-            rows_x(peer).wait_send()
-            prod_x(peer).wait_send()
-
-        def rest():
-            rows_x(peers[-1]).wait_send()
-            prod_x(peers[-1]).wait_send()
-        if_edge(rest)
+            if_there(beside[slot], lambda slot=slot: wait(omega, side_send.at[slot]))
+        gather(rows_out, rows_send)
+        gather(prod_out, prod_send)
 
 
 def near_call(n, reps, cap, coords, omega, skeleton):
@@ -491,10 +505,9 @@
             pltpu.VMEM((2, cap, leaf), bf16),
             pltpu.VMEM((2, cap, samp), bf16),
             pltpu.VMEM((leaf, samp), f32),
-            sem((3,)), sem((reps,)), sem((reps,)),
-            sem((n,)), sem((n,)), sem((n,)), sem((n,)), sem((2, 2)), sem((2, 2)),
-            sem((n,)), sem((n,)), sem((n,)), sem((n,)),
-            pltpu.SemaphoreType.REGULAR((n,)),
+            sem((3,)), sem, sem, sem, sem, sem((n,)), sem((n,)), sem((2,)), sem((2,)),
+            sem, sem, sem, sem,
+            pltpu.SemaphoreType.REGULAR((n,)), pltpu.SemaphoreType.REGULAR,
         ],
         compiler_params=pltpu.CompilerParams(collective_id=0, has_side_effects=True),
     )(coords, omega, skeleton)

time: 20 us -> 18.9 us (0.945)
  the two profiles are of different devices: /device:TPU:0 before, /device:TPU:30 now
where the time goes in v3:
time: 18.9 us; the launch traced here: 18.8 us
  Pallas kernels  18.1 us (96%)
  between operations  0.64 us (3%)
    pallas_call x1, Pallas kernels, near_call(): pl.pallas_call(functools.partial(near_kernel, n, reps, cap, sent), out_sh...  17.3 us
    pallas_call x1, Pallas kernels, finish(): pl.pallas_call(finish_kernel, out_shape=(jax.ShapeDtypeStruct(row.shape,...  0.78 us

profile of v3, /device:TPU:30, one launch (start us, length us, event | category | flops | bytes accessed | tf_op | source)
XLA Modules:
  0.0 18.8 jit_solution(15519852328076933622)
XLA Ops:
  0.6 17.3 %shard_map.50 = (f32[512,128]{1,0:T(8,128)S(1)}, f32[512,128]{1,0:T(8,128)S(1)}) custom-call(f32[3,512]{1,0:T(4,128)} %coords_in.1, bf16[512,128]{1,0:T(8,128)(2,1)} %omega_in.1, s32[1,64]{1,0:T(1,128)} %skel_in.1), custom_call_target="tpu_custom_call" | custom-call | tf_op jit(solution)/shard_map/pallas_call | solution.py:483
  18.0 0.8 %shard_map.51 = (bf16[512,128]{1,0:T(8,128)(2,1)}, f32[512,128]{1,0:T(8,128)}) custom-call(f32[512,128]{1,0:T(8,128)S(1)} %get-tuple-element.4.row, f32[512,128]{1,0:T(8,128)S(1)} %get-tuple-element.5.col), custom_call_target="tpu_custom_call" | custom-call | tf_op jit(solution)/shard_map/pallas_call | solution.py:523
